TPU v7x, 128 devices: a whole 4x4x4 slice. The times are simulated.
128 devices in a mesh: lat: 16 (over z_lo, y, core), lon: 8 (over z_hi, x).
Axes of the slice: x: 4, y: 4, z: 4 (z_hi: 2, z_lo: 2; z = z_hi * 2 + z_lo), core: 2. Of those that a mesh axis runs over, the one named last changes fastest.
Arguments:
- tokens: bfloat16 [4, 128, 256, 1024], P(None, 'lat', 'lon'), may hold values from -6 to 6
- qkv_weight: bfloat16 [3072, 1024], P(('lat', 'lon')), may hold values from -0.1875 to 0.1875
- proj_weight: bfloat16 [1024, 1024], P(('lat', 'lon')), may hold values from -0.1875 to 0.1875
- up_weight: bfloat16 [4096, 1024], P(('lat', 'lon')), may hold values from -0.1875 to 0.1875
- down_weight: bfloat16 [4096, 1024], P(('lat', 'lon')), may hold values from -0.09375 to 0.09375
- bias_table: float32 [225, 16], replicated, may hold values from -3 to 220
- sea_mask: int32 [128, 256], replicated, may hold values 0 or 1
Outputs:
- block_out: bfloat16 [4, 128, 256, 1024], P(None, 'lat', 'lon')
All inputs are finite; a program needn't handle non-finite values.
Results may differ from a plain program's by a relative error of at most 0.012.
Values may be sent and summed in bfloat16 or wider, within the bound.
No kernel may reach another device: no remote copies, remote signals or barrier semaphores. Data moves between devices by JAX's collectives and lax.ppermute only.
A program may use at most 128 MiB of HBM per device.

v0:
```python
import jax
import jax.numpy as jnp
from jax import lax
from jax.sharding import PartitionSpec as P


def from_behind(value, axis, steps):
    count = lax.axis_size(axis)
    pairs = [(source, (source + steps) % count) for source in range(count)]
    return lax.ppermute(value, axis, pairs)


def sent_together(arrays, axis, dim, along):
    ends, at = ([], 0)
    for a in arrays[:-1]:
        at += a.shape[along]
        ends.append(at)
    both = jnp.concatenate(arrays, axis=along)
    return tuple(jnp.split(lax.all_gather(both, axis, axis=dim, tiled=True), ends, axis=along))


def layer_norm(values):
    widened = values.astype(jnp.float32)
    centre = jnp.mean(widened, axis=-1, keepdims=True)
    spread = jnp.mean(jnp.square(widened - centre), axis=-1, keepdims=True)
    return ((widened - centre) * lax.rsqrt(spread + 1e-05)).astype(jnp.bfloat16)


def offsets_table():
    cell_ids = jnp.arange(64, dtype=jnp.int32)
    row_of = cell_ids // 8
    col_of = cell_ids % 8
    return (row_of[:, None] - row_of[None, :] + 7) * 15 + (col_of[:, None] - col_of[None, :] + 7)


def row_region(row_ids, total_rows):
    return jnp.where(row_ids < 4, 2, jnp.where(row_ids >= total_rows - 4, 1, 0)).astype(jnp.int32)


def window_attention(queries, pair_cells, row_start, col_start, sea_mask, pos_bias):
    batch_size, row_count, col_count, feat_width = queries.shape
    head_count = pos_bias.shape[0]
    head_size = feat_width // head_count
    lat_cells, lon_cells = sea_mask.shape
    down_count = row_count // 8
    across_count = col_count // 8
    window_count = down_count * across_count

    def to_windows(values):
        last_dim = values.shape[-1]
        shaped = values.reshape(batch_size, down_count, 8, across_count, 8, last_dim)
        return shaped.transpose(0, 1, 3, 2, 4, 5).reshape(batch_size, window_count, 64, last_dim)

    query_win = to_windows(queries)
    pair_win = to_windows(pair_cells)
    grid_rows = (row_start + jnp.arange(row_count, dtype=jnp.int32)) % lat_cells
    region = row_region(grid_rows, lat_cells).reshape(down_count, 8)
    region = jnp.broadcast_to(region[:, None, :, None], (down_count, across_count, 8, 8)).reshape(
        window_count, 64
    )
    sea_tiled = jnp.tile(sea_mask, (2, 2))
    sea_keep = lax.dynamic_slice(
        sea_tiled, (row_start % lat_cells, col_start % lon_cells), (row_count, col_count)
    )
    sea_keep = (
        sea_keep.reshape(down_count, 8, across_count, 8)
        .transpose(0, 2, 1, 3)
        .reshape(window_count, 64)
        == 1
    )
    same_cell = jnp.eye(64, dtype=bool)
    allowed = (region[:, :, None] == region[:, None, :]) & (sea_keep[:, None, :] | same_cell[None])
    group_width = 4 * head_size
    score_scale = head_size ** (-0.5)

    def one_group(group_index):
        first_col = group_index * group_width
        split_shape = (batch_size, window_count, 64, 4, head_size)
        query_part = lax.dynamic_slice_in_dim(query_win, first_col, group_width, 3).reshape(
            split_shape
        )
        key_part = lax.dynamic_slice_in_dim(pair_win, first_col, group_width, 3).reshape(
            split_shape
        )
        value_part = lax.dynamic_slice_in_dim(
            pair_win, feat_width + first_col, group_width, 3
        ).reshape(split_shape)
        bias_part = lax.dynamic_slice_in_dim(pos_bias, group_index * 4, 4, 0)
        scores = jnp.einsum(
            "bsqhd,bskhd->bshqk", query_part, key_part, preferred_element_type=jnp.float32
        )
        scores = scores * score_scale + bias_part[None, None]
        scores = jnp.where(allowed[None, :, None], scores, -1e30)
        row_top = jnp.max(scores, axis=-1, keepdims=True)
        weights = jnp.exp(scores - row_top)
        attn_probs = (weights / jnp.sum(weights, axis=-1, keepdims=True)).astype(jnp.bfloat16)
        context = jnp.einsum(
            "bshqk,bskhd->bsqhd", attn_probs, value_part, preferred_element_type=jnp.float32
        )
        return context.astype(jnp.bfloat16).reshape(batch_size, window_count, 64, group_width)

    groups = lax.map(one_group, jnp.arange(head_count // 4, dtype=jnp.int32))
    context = jnp.transpose(groups, (1, 2, 3, 0, 4)).reshape(
        batch_size, down_count, across_count, 8, 8, feat_width
    )
    return context.transpose(0, 1, 3, 2, 4, 5).reshape(batch_size, row_count, col_count, feat_width)


def per_device(tokens, qkv_weight, proj_weight, up_weight, down_weight, bias_table, sea_mask):
    batch_size, lat_rows, lon_cols, feat_width = tokens.shape
    head_count = bias_table.shape[1]
    row_base = lax.axis_index("lat") * lat_rows
    col_base = lax.axis_index("lon") * lon_cols
    offset_ids = offsets_table().reshape(-1)
    one_hot = (
        offset_ids[:, None] == jnp.arange(bias_table.shape[0], dtype=jnp.int32)[None, :]
    ).astype(jnp.float32)
    pos_bias = jnp.dot(one_hot, bias_table, precision=lax.Precision.HIGHEST)
    pos_bias = pos_bias.reshape(64, 64, head_count).transpose(2, 0, 1)
    normed = layer_norm(tokens)
    arrived = from_behind(normed[:, :4], "lat", -1)
    rolled_rows = jnp.concatenate([normed[:, 4:], arrived], axis=1)
    arrived_cols = from_behind(rolled_rows[:, :, :4], "lon", -1)
    feed_cells = jnp.concatenate([rolled_rows[:, :, 4:], arrived_cols], axis=2)
    feed_flat = feed_cells.reshape(-1, feat_width)
    projected = lax.dot_general(
        feed_flat,
        lax.all_gather(qkv_weight, ("lat", "lon"), axis=0, tiled=True),
        (((1,), (1,)), ((), ())),
        preferred_element_type=jnp.float32,
    ).astype(jnp.bfloat16)
    projected = projected.reshape(batch_size, lat_rows, lon_cols, 3 * feat_width)
    queries = projected[..., :feat_width]
    pair_cells = projected[..., feat_width:]
    rolled_context = window_attention(
        queries, pair_cells, row_base + 4, col_base + 4, sea_mask, pos_bias
    )
    came_cols = from_behind(rolled_context[:, :, lon_cols - 4 :], "lon", 1)
    back_cols = jnp.concatenate([came_cols, rolled_context[:, :, : lon_cols - 4]], axis=2)
    came_rows = from_behind(back_cols[:, lat_rows - 4 :], "lat", 1)
    context = jnp.concatenate([came_rows, back_cols[:, : lat_rows - 4]], axis=1)
    context_flat = context.reshape(-1, feat_width)
    attention_out = lax.dot_general(
        context_flat,
        lax.all_gather(proj_weight, ("lat", "lon"), axis=0, tiled=True),
        (((1,), (1,)), ((), ())),
        preferred_element_type=jnp.float32,
    )
    attended = (tokens.reshape(-1, feat_width).astype(jnp.float32) + attention_out).astype(
        jnp.bfloat16
    )
    normed_two = layer_norm(attended)
    up_part, down_part = sent_together((up_weight, down_weight), ("lat", "lon"), 0, 1)
    hidden = lax.dot_general(
        normed_two, up_part, (((1,), (1,)), ((), ())), preferred_element_type=jnp.float32
    )
    hidden = jax.nn.gelu(hidden).astype(jnp.bfloat16)
    hidden_sum = jnp.dot(hidden, down_part, preferred_element_type=jnp.float32)
    result = (attended.astype(jnp.float32) + hidden_sum).astype(jnp.bfloat16)
    return result.reshape(tokens.shape)


def solution(mesh):
    placed = (
        P(None, "lat", "lon", None),
        P(("lat", "lon"), None),
        P(("lat", "lon"), None),
        P(("lat", "lon"), None),
        P(("lat", "lon"), None),
        P(),
        P(),
    )
    return jax.shard_map(
        per_device,
        mesh=mesh,
        in_specs=placed,
        out_specs=P(None, "lat", "lon", None),
        check_vma=False,
    )
```

profile of v0, /device:TPU:1, one launch (start us, length us, event | category | flops | bytes accessed | tf_op | source)
XLA Modules:
  0.0 980.6 jit_solution(1794347280123285395)
XLA Ops:
  8.1 1.5 pad_maximum_fusion.3
  9.6 1.9 convert_reduce_fusion.1
  11.6 2.3 multiply_reduce_fusion
  14.5 1.2 fusion.79
  15.6 1.4 collective-permute-start
  17.8 2.6 fusion.48
  20.6 1.0 copy.26
  21.7 9.3 collective-permute-done
  31.1 7.6 collective-permute-start.1
  39.3 4.4 collective-permute-done.1
  44.1 274.7 %all-gather.4.cloned.1.call-done = bf16[3072,1024]{1,0:T(8,128)(2,1)} async-done(((bf16[24,1024]{1,0:T(8,128)(2,1)}), bf16[3072,1024]{1,0:T(8,128)(2,1)}) %all-gather.4.cloned.1.call-update) | async-done | bytes 6291472 | tf_op jit(solution)/shard_map/all_gather | solution.py:128
  318.8 9.7 convolution_convert_fusion.1
  328.5 1.5 copy_bitcast_fusion.2
  330.0 2.3 copy_bitcast_fusion
  332.4 45.6 %while.13 = (s32[]{:T(128)}, bf16[4,4,4,64,256]{3,4,2,1,0:T(8,128)(2,1)}, s32[4]{0:T(128)S(1)}, bf16[4,4,64,2048]{3,2,1,0:T(8,128)(2,1)}, bf16[4,4,64,1024]{3,2,...) while((s32[]{:T(128)}, ...), condition=%wide.region_5.6_spmd.clone, body=%wide.region_2.5_spmd.clone.sunk | while | flops 69255248 | bytes 12326224 | solution.py:102
  333.6 1.5 constant_dynamic-slice_fusion.6
  336.6 0.9 constant_dynamic-slice_fusion.7
  337.6 2.6 fusion.94
  340.7 2.0 convolution_convert_fusion.3
  342.7 1.1 constant_dynamic-update-slice_fusion.2
  345.0 1.5 constant_dynamic-slice_fusion.6
  348.0 0.9 constant_dynamic-slice_fusion.7
  349.0 2.6 fusion.94
  352.1 2.0 convolution_convert_fusion.3
  354.1 1.1 constant_dynamic-update-slice_fusion.2
  356.4 1.5 constant_dynamic-slice_fusion.6
  359.4 0.9 constant_dynamic-slice_fusion.7
  360.4 2.6 fusion.94
  363.5 2.0 convolution_convert_fusion.3
  365.5 1.1 constant_dynamic-update-slice_fusion.2
  367.9 1.5 constant_dynamic-slice_fusion.6
  370.8 0.9 constant_dynamic-slice_fusion.7
  371.8 2.6 fusion.94
  374.9 2.0 convolution_convert_fusion.3
  376.9 1.0 constant_dynamic-update-slice_fusion.2
  378.0 5.5 copy.28
  383.5 2.7 reshape.220
  386.2 1.8 copy_bitcast_fusion.1
  388.2 0.9 collective-permute-start.2
  389.1 10.5 %collective-permute-done.2 = bf16[4,8,4,1024]{3,2,1,0:T(4,128)(2,1)S(1)} collective-permute-done((bf16[4,8,4,1024]{3,2,1,0:T(4,128)(2,1)S(1)}, bf16[4,8,4,1024]{3,2,1,0:T(4,128)(2,1)S(1)}, u32[]{:S(2)}, u32[]{:S(2)}) %collective-permute-start.2) | collective-permute-done | bytes 262176 | tf_op jit(solution)/shard_map/ppermute | solution.py:10
  400.0 1.5 collective-permute-start.3
  401.5 11.7 %collective-permute-done.3 = bf16[4,4,32,1024]{3,2,1,0:T(8,128)(2,1)S(1)} collective-permute-done((bf16[4,4,32,1024]{3,2,1,0:T(8,128)(2,1)S(1)}, bf16[4,4,32,1024]{3,2,1,0:T(8,128)(2,1)S(1)}, u32[]{:S(2)}, u32[]{:S(2)}) %collective-permute-start.3) | collective-permute-done | bytes 1048608 | tf_op jit(solution)/shard_map/ppermute | solution.py:10
  413.3 1.8 fusion.62
  415.1 211.3 %all-gather.6.cloned.1.call-done = bf16[1024,1024]{1,0:T(8,128)(2,1)} async-done(((bf16[8,1024]{1,0:T(8,128)(2,1)}), bf16[1024,1024]{1,0:T(8,128)(2,1)}) %all-gather.6.cloned.1.call-update) | async-done | bytes 2097168 | tf_op jit(solution)/shard_map/all_gather | solution.py:145
  626.3 4.7 convert_reduce_fusion
  631.0 1.3 copy-done.4
  633.1 314.2 %all-gather.8.cloned.1.call-done = bf16[4096,2048]{1,0:T(8,128)(2,1)} async-done(((bf16[32,2048]{1,0:T(8,128)(2,1)}), bf16[4096,2048]{1,0:T(8,128)(2,1)}) %all-gather.8.cloned.1.call-update) | async-done | bytes 16777232 | tf_op jit(solution)/shard_map/all_gather | solution.py:19
  947.3 26.8 %fusion.46 = bf16[1024,1024]{1,0:T(8,128)(2,1)} fusion(bf16[1024,1024]{1,0:T(8,128)(2,1)} %copy-done.4, bf16[4096,2048]{1,0:T(8,128)(2,1)} %all-gather.8.cloned.1.call-done, f32[1024]{0:T(1024)S(1)} %add_rsqrt_fusion.1, f32[1024]{0:T(1024)S(1)} %broadcast_multiply_fusion.1), kind=kOutput, calls=%fused_computation.47 | convolution fusion | flops 17224957952 | bytes 23076864 | tf_op jit(solution)/shard_map/dot_general | solution.py:158
  (64 shorter events, 13.3 us)
Async XLA Ops:
  6.5 11.3 %copy-start = (f32[225,16]{0,1:T(8,128)S(1)}, f32[225,16]{0,1:T(8,128)}, u32[]{:S(2)}) copy-start(f32[225,16]{0,1:T(8,128)} %param.14) | copy-start | bytes 43204
  6.5 7.3 copy-start.2
  6.5 312.3 %all-gather.4.cloned.1.call-start = ((), (), s32[]{:S(2)}) async-start(), calls=%async_computation | async-start | bytes 6340608 | tf_op jit(solution)/shard_map/all_gather | solution.py:128
  7.3 619.1 %all-gather.6.cloned.1.call-start = ((), (), s32[]{:S(2)}) async-start(), calls=%async_computation.1 | async-start | bytes 2113536 | tf_op jit(solution)/shard_map/all_gather | solution.py:145
  8.0 939.3 %all-gather.8.cloned.1.call-start = ((), (), s32[]{:S(2)}) async-start(), calls=%async_computation.2 | async-start | bytes 16908288 | tf_op jit(solution)/shard_map/all_gather | solution.py:19
  13.9 3.1 copy-start.5
  15.6 15.4 %collective-permute-start = (bf16[4,4,32,1024]{3,2,1,0:T(8,128)(2,1)}, bf16[4,4,32,1024]{3,2,1,0:T(8,128)(2,1)S(1)}, u32[]{:S(2)}, u32[]{:S(2)}) collective-permute-start(bf16[4,4,32,1024]{3,2,1,0:T(8,128)(2,1)} %get-tuple-element.142), channel_id=1, source_target_pairs={{0,120},{8,0},{16,8},{24,16},{32,24},{40,32},{48,40},{56,48},{64,5... | collective-permute-start | bytes 3145736 | tf_op jit(solution)/shard_map/ppermute | solution.py:10
  31.1 12.6 %collective-permute-start.1 = (bf16[4,8,4,1024]{3,2,1,0:T(4,128)(2,1)S(1)}, bf16[4,8,4,1024]{3,2,1,0:T(4,128)(2,1)S(1)}, u32[]{:S(2)}, u32[]{:S(2)}) collective-permute-start(bf16[4,8,4,1024]{3,2,1,0:T(4,128)(2,1)S(1)} %pad_maximum_fusion.2), channel_id=1, source_target_pairs={{0,7},{1,0},{2,1},{3,2},{4,3},{5,4},{6,5},{7,6},{8,15},{9,8},{10,9... | collective-permute-start | bytes 786440 | tf_op jit(solution)/shard_map/ppermute | solution.py:10
  388.2 11.4 %collective-permute-start.2 = (bf16[4,8,4,1024]{3,2,1,0:T(4,128)(2,1)S(1)}, bf16[4,8,4,1024]{3,2,1,0:T(4,128)(2,1)S(1)}, u32[]{:S(2)}, u32[]{:S(2)}) collective-permute-start(bf16[4,8,4,1024]{3,2,1,0:T(4,128)(2,1)S(1)} %slice.46), channel_id=1, source_target_pairs={{0,1},{1,2},{2,3},{3,4},{4,5},{5,6},{6,7},{7,0},{8,9},{9,10},{10,1... | collective-permute-start | bytes 786440 | tf_op jit(solution)/shard_map/ppermute | solution.py:10
  399.6 226.7 %copy-start.3 = (bf16[4,8,32,1024]{3,2,1,0:T(8,128)(2,1)S(1)}, bf16[4,8,32,1024]{3,2,1,0:T(8,128)(2,1)}, u32[]{:S(2)}) copy-start(bf16[4,8,32,1024]{3,2,1,0:T(8,128)(2,1)} %param.9) | copy-start | bytes 6291460
  400.0 13.2 %collective-permute-start.3 = (bf16[4,4,32,1024]{3,2,1,0:T(8,128)(2,1)S(1)}, bf16[4,4,32,1024]{3,2,1,0:T(8,128)(2,1)S(1)}, u32[]{:S(2)}, u32[]{:S(2)}) collective-permute-start(bf16[4,4,32,1024]{3,2,1,0:T(8,128)(2,1)S(1)} %fusion.68), channel_id=1, source_target_pairs={{0,8},{8,16},{16,24},{24,32},{32,40},{40,48},{48,56},{56,64},{64,7... | collective-permute-start | bytes 3145736 | tf_op jit(solution)/shard_map/ppermute | solution.py:10
  631.0 1.4 copy-start.4
  947.3 26.8 %copy-start.1 = (f32[225,16]{0,1:T(8,128)S(1)}, f32[225,16]{0,1:T(8,128)}, u32[]{:S(2)}) copy-start(f32[225,16]{0,1:T(8,128)} %param.14) | copy-start | bytes 43204
Sparse Core Ops, SparseCore 0:
  9.0 309.7 all-gather.3
  320.5 305.8 all-gather.5
  628.0 319.1 all-gather.7
where the time goes:
time: 981 us
  waiting for transfers between devices  838 us (85%)
  matrix products  62.2 us (6%)
  local copies, waits for them, and re-layouts  39.9 us (4%)
  between operations  13.3 us (1%)
  starting transfers between devices  11.5 us (1%)
  other arithmetic  10.9 us (1%)
    all_gather x1, waiting for transfers between devices, sent_together(): lax.all_gather(both, axis, axis=dim, tiled=True)  314 us
    all_gather x1, waiting for transfers between devices, per_device(): lax.all_gather(qkv_weight, ('lat', 'lon'), axis=0, tiled=True)  275 us
    all_gather x1, waiting for transfers between devices, per_device(): lax.all_gather(proj_weight, ('lat', 'lon'), axis=0, tiled=True)  211 us
    ppermute x4, waiting for transfers between devices, from_behind(): return lax.ppermute(value, axis, pairs)  36 us
    dot_general x1, matrix products, per_device(): hidden_sum = jnp.dot(hidden, down_part, preferred_element_type=jnp.float32)  26.8 us
  transfers between devices with their start and end apart: 7, of which 7 were waited for; matrix products, arithmetic and copies ran while one was open for 9% of the time, Pallas kernels for 0%

commit v1 on v0

--- a/solution.py
+++ b/solution.py
@@ -2,6 +2,11 @@
 import jax.numpy as jnp
 from jax import lax
 from jax.sharding import PartitionSpec as P
+
+
+def gather_over(x, mesh_axis, dim):
+    outgoing = jnp.stack([x] * lax.axis_size(mesh_axis))
+    return jnp.concatenate(lax.all_to_all(outgoing, mesh_axis, 0, 0), axis=dim)
 
 
 def from_behind(value, axis, steps):
@@ -125,7 +130,7 @@
     feed_flat = feed_cells.reshape(-1, feat_width)
     projected = lax.dot_general(
         feed_flat,
-        lax.all_gather(qkv_weight, ("lat", "lon"), axis=0, tiled=True),
+        gather_over(qkv_weight, ("lat", "lon"), 0),
         (((1,), (1,)), ((), ())),
         preferred_element_type=jnp.float32,
     ).astype(jnp.bfloat16)

time: 981 us -> 721 us (0.73)
  waiting for transfers between devices: 838 us -> 565 us
  starting transfers between devices: 11.5 us -> 21.8 us
    all_gather x1 -> x0, waiting for transfers between devices: 275 us -> none  [per_device(): lax.all_gather(qkv_weight, ('lat', 'lon'), axis=0, tiled=True)]
    ppermute x4, waiting for transfers between devices: 36 us -> 101 us  [from_behind(): return lax.ppermute(value, axis, pairs)]
    all_gather x1, waiting for transfers between devices: 211 us -> 149 us  [per_device(): lax.all_gather(proj_weight, ('lat', 'lon'), axis=0, tiled=True)]
    all_to_all x0 -> x1, starting transfers between devices: none -> 11.9 us  [gather_over(): return jnp.concatenate(lax.all_to_all(outgoing, mesh_axis, 0, 0), axis=dim)]
  transfers between devices with their start and end apart: 7 -> 7, of which waited for: 7 -> 6; matrix products, arithmetic and copies ran while one was open for 9% -> 12% of each run, Pallas kernels for 0% -> 0%
where the time goes in v1:
time: 721 us; the launch traced here: 720 us
  waiting for transfers between devices  565 us (78%)
  matrix products  62.2 us (9%)
  local copies, waits for them, and re-layouts  44.2 us (6%)
  starting transfers between devices  21.8 us (3%)
  between operations  13.6 us (2%)
  other arithmetic  7.69 us (1%)
    all_gather x1, waiting for transfers between devices, sent_together(): lax.all_gather(both, axis, axis=dim, tiled=True)  314 us
    all_gather x1, waiting for transfers between devices, per_device(): lax.all_gather(proj_weight, ('lat', 'lon'), axis=0, tiled=True)  149 us
    ppermute x4, waiting for transfers between devices, from_behind(): return lax.ppermute(value, axis, pairs)  101 us
    dot_general x1, matrix products, per_device(): hidden_sum = jnp.dot(hidden, down_part, preferred_element_type=jnp.float32)  26.8 us
  transfers between devices with their start and end apart: 7, of which 6 were waited for; matrix products, arithmetic and copies ran while one was open for 12% of the time, Pallas kernels for 0%

profile of v1, /device:TPU:1, one launch (start us, length us, event | category | flops | bytes accessed | tf_op | source)
XLA Modules:
  0.0 720.2 jit_solution(15055308636836806585)
XLA Ops:
  6.5 0.7 all-gather.3.cloned.1.call-update
  7.3 1.5 pad_maximum_fusion.3
  8.9 4.2 stack.2
  13.1 11.9 %all-to-all-start = ((bf16[128,24,1024]{2,1,0:T(8,128)(2,1)}), bf16[128,24,1024]{2,1,0:T(8,128)(2,1)}, u32[]{:S(2)}, u32[]{:S(2)}) async-start(bf16[128,24,1024]{2,1,0:T(8,128)(2,1)} %stack.2), calls=%async_computation | async-start | bytes 12582912 | tf_op jit(solution)/shard_map/all_to_all | solution.py:9
  25.4 0.7 multiply_reduce_fusion
  26.7 1.2 fusion.79
  27.8 1.1 collective-permute-start
  29.8 2.6 fusion.48
  32.6 1.0 copy.26
  33.6 76.9 %collective-permute-done = bf16[4,4,32,1024]{3,2,1,0:T(8,128)(2,1)S(1)} collective-permute-done((bf16[4,4,32,1024]{3,2,1,0:T(8,128)(2,1)}, bf16[4,4,32,1024]{3,2,1,0:T(8,128)(2,1)S(1)}, u32[]{:S(2)}, u32[]{:S(2)}) %collective-permute-start) | collective-permute-done | bytes 1048608 | tf_op jit(solution)/shard_map/ppermute | solution.py:15
  110.6 6.6 collective-permute-start.1
  117.8 2.8 collective-permute-done.1
  121.0 9.7 %convolution_convert_fusion.1 = bf16[1024,3072]{1,0:T(8,128)(2,1)S(1)} fusion(bf16[1024,1024]{1,0:T(8,128)(2,1)S(1)} %bitcast.74, bf16[3072,1024]{1,0:T(8,128)(2,1)} %bitcast.2), kind=kOutput, calls=%fused_computation.42 | convolution fusion | flops 6445596672 | bytes 14680064 | tf_op jit(solution)/shard_map/dot_general | solution.py:131
  130.7 1.5 copy_bitcast_fusion.2
  132.2 2.3 copy_bitcast_fusion
  134.6 45.6 %while.13 = (s32[]{:T(128)}, bf16[4,4,4,64,256]{3,4,2,1,0:T(8,128)(2,1)}, s32[4]{0:T(128)S(1)}, bf16[4,4,64,2048]{3,2,1,0:T(8,128)(2,1)}, bf16[4,4,64,1024]{3,2,...) while((s32[]{:T(128)}, ...), condition=%wide.region_5.6_spmd.clone, body=%wide.region_2.5_spmd.clone.sunk | while | flops 69255248 | bytes 12326224 | solution.py:107
  135.8 1.5 constant_dynamic-slice_fusion.6
  138.7 0.9 constant_dynamic-slice_fusion.7
  139.8 2.6 fusion.94
  142.8 2.0 convolution_convert_fusion.3
  144.9 1.1 constant_dynamic-update-slice_fusion.2
  147.2 1.5 constant_dynamic-slice_fusion.6
  150.2 0.9 constant_dynamic-slice_fusion.7
  151.2 2.6 fusion.94
  154.3 2.0 convolution_convert_fusion.3
  156.3 1.1 constant_dynamic-update-slice_fusion.2
  158.6 1.5 constant_dynamic-slice_fusion.6
  161.6 0.9 constant_dynamic-slice_fusion.7
  162.6 2.6 fusion.94
  165.7 2.0 convolution_convert_fusion.3
  167.7 1.1 constant_dynamic-update-slice_fusion.2
  170.0 1.5 constant_dynamic-slice_fusion.6
  172.9 0.9 constant_dynamic-slice_fusion.7
  174.0 2.6 fusion.94
  177.1 2.0 convolution_convert_fusion.3
  179.1 1.1 constant_dynamic-update-slice_fusion.2
  180.1 5.5 copy.28
  185.7 2.7 reshape.226
  188.4 1.8 copy_bitcast_fusion.1
  190.4 9.5 %collective-permute-done.2 = bf16[4,8,4,1024]{3,2,1,0:T(4,128)(2,1)S(1)} collective-permute-done((bf16[4,8,4,1024]{3,2,1,0:T(4,128)(2,1)S(1)}, bf16[4,8,4,1024]{3,2,1,0:T(4,128)(2,1)S(1)}, u32[]{:S(2)}, u32[]{:S(2)}) %collective-permute-start.2) | collective-permute-done | bytes 262176 | tf_op jit(solution)/shard_map/ppermute | solution.py:15
  200.4 2.1 collective-permute-start.3
  202.5 11.7 %collective-permute-done.3 = bf16[4,4,32,1024]{3,2,1,0:T(8,128)(2,1)S(1)} collective-permute-done((bf16[4,4,32,1024]{3,2,1,0:T(8,128)(2,1)S(1)}, bf16[4,4,32,1024]{3,2,1,0:T(8,128)(2,1)S(1)}, u32[]{:S(2)}, u32[]{:S(2)}) %collective-permute-start.3) | collective-permute-done | bytes 1048608 | tf_op jit(solution)/shard_map/ppermute | solution.py:15
  214.2 1.8 fusion.62
  216.0 149.3 %all-gather.3.cloned.1.call-done = bf16[1024,1024]{1,0:T(8,128)(2,1)} async-done(((bf16[8,1024]{1,0:T(8,128)(2,1)}), bf16[1024,1024]{1,0:T(8,128)(2,1)}) %all-gather.3.cloned.1.call-update) | async-done | bytes 2097168 | tf_op jit(solution)/shard_map/all_gather | solution.py:150
  365.3 4.7 convert_reduce_fusion
  370.0 1.3 copy-done.4
  372.0 314.5 %all-gather.5.cloned.1.call-done = bf16[4096,2048]{1,0:T(8,128)(2,1)} async-done(((bf16[32,2048]{1,0:T(8,128)(2,1)}), bf16[4096,2048]{1,0:T(8,128)(2,1)}) %all-gather.5.cloned.1.call-update) | async-done | bytes 16777232 | tf_op jit(solution)/shard_map/all_gather | solution.py:24
  686.5 26.8 %fusion.46 = bf16[1024,1024]{1,0:T(8,128)(2,1)} fusion(bf16[1024,1024]{1,0:T(8,128)(2,1)} %copy-done.4, bf16[4096,2048]{1,0:T(8,128)(2,1)} %all-gather.5.cloned.1.call-done, f32[1024]{0:T(1024)S(1)} %add_rsqrt_fusion.1, f32[1024]{0:T(1024)S(1)} %broadcast_multiply_fusion.1), kind=kOutput, calls=%fused_computation.47 | convolution fusion | flops 17224957952 | bytes 23076864 | tf_op jit(solution)/shard_map/dot_general | solution.py:163
  (64 shorter events, 12.4 us)
Async XLA Ops:
  6.5 23.3 %copy-start = (f32[225,16]{0,1:T(8,128)S(1)}, f32[225,16]{0,1:T(8,128)}, u32[]{:S(2)}) copy-start(f32[225,16]{0,1:T(8,128)} %param.14) | copy-start | bytes 43204
  6.5 358.8 %all-gather.3.cloned.1.call-start = ((), (), s32[]{:S(2)}) async-start(), calls=%async_computation.1 | async-start | bytes 2113536 | tf_op jit(solution)/shard_map/all_gather | solution.py:150
  7.3 679.3 %all-gather.5.cloned.1.call-start = ((), (), s32[]{:S(2)}) async-start(), calls=%async_computation.2 | async-start | bytes 16908288 | tf_op jit(solution)/shard_map/all_gather | solution.py:24
  13.1 11.9 %copy-start.2 = (bf16[4,8,32,1024]{3,2,1,0:T(8,128)(2,1)S(1)}, bf16[4,8,32,1024]{3,2,1,0:T(8,128)(2,1)}, u32[]{:S(2)}) copy-start(bf16[4,8,32,1024]{3,2,1,0:T(8,128)(2,1)} %param.9) | copy-start | bytes 6291460
  13.1 107.8 %all-to-all-start = ((bf16[128,24,1024]{2,1,0:T(8,128)(2,1)}), bf16[128,24,1024]{2,1,0:T(8,128)(2,1)}, u32[]{:S(2)}, u32[]{:S(2)}) async-start(bf16[128,24,1024]{2,1,0:T(8,128)(2,1)} %stack.2), calls=%async_computation | async-start | bytes 12582912 | tf_op jit(solution)/shard_map/all_to_all | solution.py:9
  26.1 2.9 copy-start.5
  27.8 82.7 %collective-permute-start = (bf16[4,4,32,1024]{3,2,1,0:T(8,128)(2,1)}, bf16[4,4,32,1024]{3,2,1,0:T(8,128)(2,1)S(1)}, u32[]{:S(2)}, u32[]{:S(2)}) collective-permute-start(bf16[4,4,32,1024]{3,2,1,0:T(8,128)(2,1)} %get-tuple-element.142), channel_id=1, source_target_pairs={{0,120},{8,0},{16,8},{24,16},{32,24},{40,32},{48,40},{56,48},{64,5... | collective-permute-start | bytes 3145736 | tf_op jit(solution)/shard_map/ppermute | solution.py:15
  110.6 9.9 %collective-permute-start.1 = (bf16[4,8,4,1024]{3,2,1,0:T(4,128)(2,1)S(1)}, bf16[4,8,4,1024]{3,2,1,0:T(4,128)(2,1)S(1)}, u32[]{:S(2)}, u32[]{:S(2)}) collective-permute-start(bf16[4,8,4,1024]{3,2,1,0:T(4,128)(2,1)S(1)} %pad_maximum_fusion.2), channel_id=1, source_target_pairs={{0,7},{1,0},{2,1},{3,2},{4,3},{5,4},{6,5},{7,6},{8,15},{9,8},{10,9... | collective-permute-start | bytes 786440 | tf_op jit(solution)/shard_map/ppermute | solution.py:15
  190.4 9.6 %collective-permute-start.2 = (bf16[4,8,4,1024]{3,2,1,0:T(4,128)(2,1)S(1)}, bf16[4,8,4,1024]{3,2,1,0:T(4,128)(2,1)S(1)}, u32[]{:S(2)}, u32[]{:S(2)}) collective-permute-start(bf16[4,8,4,1024]{3,2,1,0:T(4,128)(2,1)S(1)} %slice.46), channel_id=1, source_target_pairs={{0,1},{1,2},{2,3},{3,4},{4,5},{5,6},{6,7},{7,0},{8,9},{9,10},{10,1... | collective-permute-start | bytes 786440 | tf_op jit(solution)/shard_map/ppermute | solution.py:15
  200.0 165.4 %copy-start.3 = (bf16[4,8,32,1024]{3,2,1,0:T(8,128)(2,1)S(1)}, bf16[4,8,32,1024]{3,2,1,0:T(8,128)(2,1)}, u32[]{:S(2)}) copy-start(bf16[4,8,32,1024]{3,2,1,0:T(8,128)(2,1)} %param.9) | copy-start | bytes 6291460
  200.4 13.8 %collective-permute-start.3 = (bf16[4,4,32,1024]{3,2,1,0:T(8,128)(2,1)S(1)}, bf16[4,4,32,1024]{3,2,1,0:T(8,128)(2,1)S(1)}, u32[]{:S(2)}, u32[]{:S(2)}) collective-permute-start(bf16[4,4,32,1024]{3,2,1,0:T(8,128)(2,1)S(1)} %fusion.68), channel_id=1, source_target_pairs={{0,8},{8,16},{16,24},{24,32},{32,40},{40,48},{48,56},{56,64},{64,7... | collective-permute-start | bytes 3145736 | tf_op jit(solution)/shard_map/ppermute | solution.py:15
  370.0 1.4 copy-start.4
  686.5 26.8 %copy-start.1 = (f32[225,16]{0,1:T(8,128)S(1)}, f32[225,16]{0,1:T(8,128)}, u32[]{:S(2)}) copy-start(f32[225,16]{0,1:T(8,128)} %param.14) | copy-start | bytes 43204
Sparse Core Ops, SparseCore 0:
  9.0 356.2 all-gather.2
  367.0 319.4 all-gather.4
